TPU v7x, 32 devices: a whole 2x2x4 slice. The times are simulated.
32 devices in a mesh: groups: 2 (over x), tensor: 16 (over z, y, core).
Axes of the slice: x: 2, y: 2, z: 4, core: 2. Of those that a mesh axis runs over, the one named last changes fastest.
Arguments:
- video_state: float32 [128, 4096], P(('groups', 'tensor')), parts along dimension 0, may hold values from -54 to 54
- audio_state: float32 [128, 2048], P(('groups', 'tensor')), parts along dimension 0, may hold values from -54 to 54
- video_modulation: float32 [12, 4096], P('groups'), parts along dimension 0, may hold values from -3 to 3
- audio_modulation: float32 [12, 2048], P('groups'), parts along dimension 0, may hold values from -3 to 3
- video_query: bfloat16 [4096, 2048], P(None, 'tensor'), may hold values from -0.09375 to 0.09375
- audio_keyval: bfloat16 [2048, 2, 2048], P(None, None, 'tensor'), may hold values from -0.125 to 0.125
- video_output: bfloat16 [2048, 4096], P('tensor'), may hold values from -0.125 to 0.125
- audio_query: bfloat16 [2048, 2048], P(None, 'tensor'), may hold values from -0.125 to 0.125
- video_keyval: bfloat16 [4096, 2, 2048], P(None, None, 'tensor'), may hold values from -0.09375 to 0.09375
- audio_output: bfloat16 [2048, 2048], P('tensor'), may hold values from -0.125 to 0.125
- video_expand: bfloat16 [4096, 16384], P(None, 'tensor'), may hold values from -0.09375 to 0.09375
- video_shrink: bfloat16 [16384, 4096], P('tensor'), may hold values from -0.046875 to 0.046875
- audio_expand: bfloat16 [2048, 8192], P(None, 'tensor'), may hold values from -0.125 to 0.125
- audio_shrink: bfloat16 [8192, 2048], P('tensor'), may hold values from -0.0625 to 0.0625
Outputs:
- video_next: float32 [128, 4096], P(('groups', 'tensor')), parts along dimension 0
- audio_next: float32 [128, 2048], P(('groups', 'tensor')), parts along dimension 0
There are 2 independent parts, one for each index of `groups`. A program takes and returns all parts, laid end to end along the dimension named above; an argument that names none is the same for every part. Nothing has to cross between parts.
All inputs are finite; a program needn't handle non-finite values.
Results may differ from a plain program's by a relative error of at most 0.0029.
Values may be sent and summed in bfloat16 or wider, within the bound.
A program may use at most 64 MiB of HBM per device.

v0:
```python
import jax
import jax.numpy as jnp
from jax import lax
from jax.sharding import PartitionSpec as P

HEAD_DIM = 64
epsilon = 1e-06


def partner(block, axis, distance):
    count = lax.axis_size(axis)
    route = []
    for low in range(count):
        high = low | 1 << distance
        if high != low and high < count:
            route += [(low, high), (high, low)]
    return lax.ppermute(block, axis, route)


def modulate(states, modulation, first):
    normed = states * lax.rsqrt(jnp.mean(states * states, axis=-1, keepdims=True) + epsilon)
    return (normed * (1.0 + modulation[first + 1]) + modulation[first]).astype(jnp.bfloat16)


def head_normalize(tensor):
    values = tensor.astype(jnp.float32)
    return (values * lax.rsqrt(jnp.mean(values * values, axis=-1, keepdims=True) + epsilon)).astype(
        jnp.bfloat16
    )


def softmax_weights(scores):
    expo = jnp.exp(scores)
    return (expo / jnp.sum(expo, axis=-1, keepdims=True)).astype(jnp.bfloat16)


def local_heads(queries, key_part, value_part):
    query_count, width = queries.shape
    source_count = key_part.shape[0]
    head_count = width // HEAD_DIM
    query_hat = head_normalize(queries.reshape(query_count, head_count, HEAD_DIM))
    key_hat = head_normalize(key_part.reshape(source_count, head_count, HEAD_DIM))
    scores = jnp.einsum(
        "qhd,khd->hqk", query_hat, key_hat, preferred_element_type=jnp.float32
    ) * HEAD_DIM ** (-0.5)
    weights = softmax_weights(scores)
    values = value_part.reshape(source_count, head_count, HEAD_DIM)
    mixed = jnp.einsum("hqk,khd->qhd", weights, values, preferred_element_type=jnp.float32)
    return mixed.astype(jnp.bfloat16).reshape(query_count, width)


def project_attend(query_rows, source_rows, query_weight, keyval_weight):
    width = query_weight.shape[1]
    queries = jnp.dot(query_rows, query_weight, preferred_element_type=jnp.float32).astype(
        jnp.bfloat16
    )
    flat_weight = keyval_weight.reshape(keyval_weight.shape[0], 2 * width)
    keyvals = jnp.dot(source_rows, flat_weight, preferred_element_type=jnp.float32).astype(
        jnp.bfloat16
    )
    key_part = keyvals[:, :width]
    value_part = keyvals[:, width:]
    if width >= HEAD_DIM:
        return local_heads(queries, key_part, value_part)
    query_float = queries.astype(jnp.float32)
    key_float = key_part.astype(jnp.float32)
    query_square = jnp.sum(query_float * query_float, axis=1, keepdims=True)
    key_square = jnp.sum(key_float * key_float, axis=1, keepdims=True)
    other_query, other_key = partner((query_square, key_square), "tensor", 0)
    query_hat = (query_float * lax.rsqrt((query_square + other_query) / HEAD_DIM + epsilon)).astype(
        jnp.bfloat16
    )
    key_hat = (key_float * lax.rsqrt((key_square + other_key) / HEAD_DIM + epsilon)).astype(
        jnp.bfloat16
    )
    partial_scores = jnp.einsum("qd,kd->qk", query_hat, key_hat, preferred_element_type=jnp.float32)
    other_scores = partner(partial_scores, "tensor", 0)
    scores = (partial_scores + other_scores) * HEAD_DIM ** (-0.5)
    weights = softmax_weights(scores)
    return jnp.dot(weights, value_part, preferred_element_type=jnp.float32).astype(jnp.bfloat16)


def output_rows(mixed, weight):
    return jnp.dot(mixed, weight, preferred_element_type=jnp.float32)


def feed_rows(inputs, expand, shrink):
    hidden = jnp.dot(inputs, expand, preferred_element_type=jnp.float32)
    hidden = jax.nn.gelu(hidden, approximate=True).astype(jnp.bfloat16)
    return jnp.dot(hidden, shrink, preferred_element_type=jnp.float32)


def on_device(
    video_state,
    audio_state,
    video_modulation,
    audio_modulation,
    video_query,
    audio_keyval,
    video_output,
    audio_query,
    video_keyval,
    audio_output,
    video_expand,
    video_shrink,
    audio_expand,
    audio_shrink,
):
    video_count = video_state.shape[0]
    audio_own = modulate(audio_state, audio_modulation, 0)
    video_whole = lax.all_gather(video_state, "tensor", axis=0, tiled=True)
    video_normed = modulate(video_whole, video_modulation, 0)
    audio_normed = lax.all_gather(audio_own, "tensor", axis=0, tiled=True)
    video_mixed = project_attend(video_normed, audio_normed, video_query, audio_keyval)
    audio_mixed = project_attend(audio_normed, video_normed, audio_query, video_keyval)
    audio_term = lax.psum_scatter(
        output_rows(audio_mixed, audio_output), "tensor", scatter_dimension=0, tiled=True
    )
    audio_mid = audio_state + audio_modulation[2] * audio_term
    audio_inner_own = modulate(audio_mid, audio_modulation, 3)
    partial_term = jnp.dot(video_mixed, video_output, preferred_element_type=jnp.float32)
    full_term = lax.psum(partial_term, "tensor")
    video_mid_whole = video_whole + video_modulation[2] * full_term
    video_inner = modulate(video_mid_whole, video_modulation, 3)
    first_row = lax.axis_index("tensor") * video_count
    video_mid = lax.dynamic_slice_in_dim(video_mid_whole, first_row, video_count, 0)
    audio_inner = lax.all_gather(audio_inner_own, "tensor", axis=0, tiled=True)
    video_feed = lax.psum_scatter(
        feed_rows(video_inner, video_expand, video_shrink),
        "tensor",
        scatter_dimension=0,
        tiled=True,
    )
    audio_feed = lax.psum_scatter(
        feed_rows(audio_inner, audio_expand, audio_shrink),
        "tensor",
        scatter_dimension=0,
        tiled=True,
    )
    video_next = video_mid + video_modulation[5] * video_feed
    audio_next = audio_mid + audio_modulation[5] * audio_feed
    return (video_next, audio_next)


def solution(mesh):
    placed = (
        P(("groups", "tensor"), None),
        P(("groups", "tensor"), None),
        P("groups", None),
        P("groups", None),
        P(None, "tensor"),
        P(None, None, "tensor"),
        P("tensor", None),
        P(None, "tensor"),
        P(None, None, "tensor"),
        P("tensor", None),
        P(None, "tensor"),
        P("tensor", None),
        P(None, "tensor"),
        P("tensor", None),
    )
    return jax.shard_map(
        on_device,
        mesh=mesh,
        in_specs=placed,
        out_specs=(P(("groups", "tensor"), None), P(("groups", "tensor"), None)),
        check_vma=False,
    )
```

profile of v0, /device:TPU:0, one launch (start us, length us, event | category | flops | bytes accessed | tf_op | source)
XLA Modules:
  0.0 302.8 jit_solution(14228679446785322309)
XLA Ops:
  7.2 0.7 all-gather.5.cloned.1.call-update
  8.0 1.8 fusion.80
  9.7 0.9 multiply_reduce_fusion.7
  10.6 0.8 fusion.54
  11.5 24.0 %all-gather.1 = bf16[16,4,2048]{2,1,0:T(4,128)(2,1)S(1)} all-gather(bf16[1,4,2048]{2,1,0:T(4,128)(2,1)S(1)} %fusion.54), channel_id=1, replica_groups=mesh['groups'=2,'tensor'=16] {'tensor'}, dimensions={0}, use_global_device_ids=true | all-gather | bytes 278528 | tf_op jit(solution)/shard_map/all_gather | solution.py:113
  35.5 1.3 fusion.9
  36.9 1.5 convolution_convert_fusion.2
  38.6 0.7 copy.50
  39.6 0.7 fusion.79
  40.3 10.6 %all-gather.5.cloned.1.call-done = f32[16,4,4096]{2,1,0:T(4,128)} async-done(((f32[1,4,4096]{2,1,0:T(4,128)}), f32[16,4,4096]{2,1,0:T(4,128)}) %all-gather.5.cloned.1.call-update) | async-done | bytes 1048592 | tf_op jit(solution)/shard_map/all_gather | solution.py:111
  50.9 1.6 reshape.111
  52.5 0.2 multiply_reduce_fusion.1
  52.7 2.1 fusion.5
  55.2 0.7 copy.51
  55.9 1.6 fusion.8
  57.8 0.2 multiply_convert_fusion
  58.1 0.9 convolution_convert_fusion
  59.0 2.1 fusion.84
  61.2 0.2 multiply_convert_fusion.2
  61.6 0.9 convolution_convert_fusion.1
  62.5 2.6 fusion.83
  65.2 0.6 dynamic-slice
  66.4 93.9 %all-reduce.10.cloned.1.call-done = (f32[64,4096]{1,0:T(8,128)}, f32[64,2048]{1,0:T(8,128)}) async-done(((f32[64,4096]{1,0:T(8,128)}, f32[64,2048]{1,0:T(8,128)}), (f32[64,4096]{1,0:T(8,128)}, f32[64,2048]{1,0:T(8,128)})) %all-reduce.10.cloned.1.call-update) | async-done | bytes 1572880 | tf_op jit(solution)/shard_map/psum | solution.py:122
  160.3 1.0 multiply_reduce_fusion.6
  161.4 21.4 %all-gather.2 = bf16[16,4,2048]{2,1,0:T(4,128)(2,1)} all-gather(bf16[1,4,2048]{2,1,0:T(4,128)(2,1)S(1)} %fusion.55), channel_id=1, replica_groups=mesh['groups'=2,'tensor'=16] {'tensor'}, dimensions={0}, use_global_device_ids=true | all-gather | bytes 278528 | tf_op jit(solution)/shard_map/all_gather | solution.py:127
  182.8 1.0 reshape.115
  183.8 2.5 multiply_reduce_fusion
  186.4 3.4 %fusion.37 = f32[64,2048]{1,0:T(8,128)} fusion(bf16[512,2048]{1,0:T(8,128)(2,1)S(1)} %copy-done, bf16[64,2048]{1,0:T(8,128)(2,1)S(1)} %reshape.115, bf16[2048,512]{1,0:T(8,128)(2,1)} %param.26), kind=kOutput, calls=%fused_computation.49 | convolution fusion | flops 268730368 | bytes 4980736 | tf_op jit(solution)/shard_map/dot_general | solution.py:90
  189.8 9.9 %fusion.24 = f32[64,4096]{1,0:T(8,128)} fusion(bf16[1024,4096]{1,0:T(8,128)(2,1)} %param.25, bf16[4096,1024]{1,0:T(8,128)(2,1)} %param.24, f32[64,4096]{1,0:T(8,128)S(1)} %copy-done.1, f32[4096]{0:T(1024)S(1)} %bitcast.60, f32[4096]{0:T(1024)S(1)} %bitcast.61, f32[64]{0:T(128)S(1)} %add_rsqrt_fusion.5), kind=kOutput, calls=%fused_computation.35 | convolution fusion | flops 1075380224 | bytes 18907392 | tf_op jit(solution)/shard_map/dot_general | solution.py:90
  199.8 93.4 %all-reduce.8.cloned.1.call-done = (f32[64,4096]{1,0:T(8,128)}, f32[64,2048]{1,0:T(8,128)}) async-done(((f32[64,4096]{1,0:T(8,128)}, f32[64,2048]{1,0:T(8,128)}), (f32[64,4096]{1,0:T(8,128)}, f32[64,2048]{1,0:T(8,128)})) %all-reduce.8.cloned.1.call-update) | async-done | bytes 1572880
  293.2 1.5 fusion.44
  294.7 1.6 fusion.39
  (55 shorter events, 1.7 us)
Async XLA Ops:
  7.2 179.2 %copy-start = (bf16[512,2048]{1,0:T(8,128)(2,1)S(1)}, bf16[512,2048]{1,0:T(8,128)(2,1)}, u32[]{:S(2)}) copy-start(bf16[512,2048]{1,0:T(8,128)(2,1)} %param.27) | copy-start | bytes 6291460
  7.2 32.4 %copy-start.3 = (f32[6,4096]{1,0:T(8,128)S(1)}, f32[6,4096]{1,0:T(8,128)}, u32[]{:S(2)}) copy-start(f32[6,4096]{1,0:T(8,128)} %param.16) | copy-start | bytes 294916
  7.2 43.8 %all-gather.5.cloned.1.call-start = ((), (), s32[]{:S(2)}) async-start(), calls=%async_computation | async-start | bytes 1114112 | tf_op jit(solution)/shard_map/all_gather | solution.py:111
  7.9 152.4 %all-reduce.10.cloned.1.call-start = ((), (), s32[]{:S(2)}) async-start(), calls=%async_computation.2 | async-start | bytes 3145728 | tf_op jit(solution)/shard_map/psum | solution.py:122
  40.3 14.5 %copy-start.4 = (f32[1,4096]{1,0:T(1,128)}, f32[1,4096]{1,0:T(1,128)S(1)}, u32[]{:S(2)}) copy-start(f32[1,4096]{1,0:T(1,128)S(1)} %get-tuple-element.11) | copy-start | bytes 49156
  40.3 14.6 %copy-start.5 = (f32[1,4096]{1,0:T(1,128)}, f32[1,4096]{1,0:T(1,128)S(1)}, u32[]{:S(2)}) copy-start(f32[1,4096]{1,0:T(1,128)S(1)} %get-tuple-element.12) | copy-start | bytes 49156
  61.4 3.8 %copy-start.13 = (u32[32]{0:T(128)S(1)}, u32[32]{0:T(128)}, u32[]{:S(2)}) copy-start(u32[32]{0:T(128)} %constant.50) | copy-start | bytes 388
  61.4 99.0 %copy-start.2 = (f32[4,2048]{1,0:T(4,128)S(1)}, f32[4,2048]{1,0:T(4,128)}, u32[]{:S(2)}) copy-start(f32[4,2048]{1,0:T(4,128)} %param.15) | copy-start | bytes 98308
  61.4 98.9 %copy-start.12 = (f32[1,2048]{1,0:T(1,128)S(1)}, f32[1,2048]{1,0:T(1,128)}, u32[]{:S(2)}) copy-start(f32[1,2048]{1,0:T(1,128)} %get-tuple-element.17) | copy-start | bytes 24580
  61.5 99.8 %copy-start.10 = (f32[1,2048]{1,0:T(1,128)S(1)}, f32[1,2048]{1,0:T(1,128)}, u32[]{:S(2)}) copy-start(f32[1,2048]{1,0:T(1,128)} %get-tuple-element.20) | copy-start | bytes 24580
  61.6 99.8 %copy-start.11 = (f32[1,2048]{1,0:T(1,128)S(1)}, f32[1,2048]{1,0:T(1,128)}, u32[]{:S(2)}) copy-start(f32[1,2048]{1,0:T(1,128)} %get-tuple-element.21) | copy-start | bytes 24580
  65.1 228.1 %all-reduce.8.cloned.1.call-start = ((), (), s32[]{:S(2)}) async-start(), calls=%async_computation.1 | async-start | bytes 3145728
  186.3 3.4 %copy-start.1 = (f32[64,4096]{1,0:T(8,128)S(1)}, f32[64,4096]{1,0:T(8,128)}, u32[]{:S(2)}) copy-start(f32[64,4096]{1,0:T(8,128)} %get-tuple-element.9) | copy-start | bytes 3145732
  186.3 3.4 %copy-start.7 = (f32[1,4096]{1,0:T(1,128)S(1)}, f32[1,4096]{1,0:T(1,128)}, u32[]{:S(2)}) copy-start(f32[1,4096]{1,0:T(1,128)} %get-tuple-element.14) | copy-start | bytes 49156
  186.3 3.4 %copy-start.8 = (f32[1,4096]{1,0:T(1,128)S(1)}, f32[1,4096]{1,0:T(1,128)}, u32[]{:S(2)}) copy-start(f32[1,4096]{1,0:T(1,128)} %get-tuple-element.15) | copy-start | bytes 49156
  189.8 103.4 %copy-start.9 = (f32[1,2048]{1,0:T(1,128)S(1)}, f32[1,2048]{1,0:T(1,128)}, u32[]{:S(2)}) copy-start(f32[1,2048]{1,0:T(1,128)} %get-tuple-element.16) | copy-start | bytes 24580
  189.8 104.9 %copy-start.6 = (f32[1,4096]{1,0:T(1,128)S(1)}, f32[1,4096]{1,0:T(1,128)}, u32[]{:S(2)}) copy-start(f32[1,4096]{1,0:T(1,128)} %get-tuple-element.10) | copy-start | bytes 49156
Sparse Core Ops, SparseCore 0:
  10.2 40.7 all-gather.4
  65.2 95.0 all-reduce.9
  199.9 93.2 all-reduce.7
where the time goes:
time: 304 us; the launch traced here: 303 us
  waiting for transfers between devices  199 us (65%)
  blocking collectives  45.4 us (15%)
  matrix products  26.7 us (9%)
  between operations  14.8 us (5%)
  other arithmetic  12 us (4%)
  local copies, waits for them, and re-layouts  5.14 us (2%)
    unnamed x4, waiting for transfers between devices  94.1 us
    psum x1, waiting for transfers between devices, on_device(): full_term = lax.psum(partial_term, 'tensor')  93.9 us
    all_gather x1, blocking collectives, on_device(): audio_normed = lax.all_gather(audio_own, 'tensor', axis=0, tiled=True)  24 us
    all_gather x1, blocking collectives, on_device(): audio_inner = lax.all_gather(audio_inner_own, 'tensor', axis=0, tiled=True)  21.4 us
    dot_general x2, matrix products, feed_rows(): return jnp.dot(hidden, shrink, preferred_element_type=jnp.float32)  13.4 us
    all_gather x1, waiting for transfers between devices, on_device(): video_whole = lax.all_gather(video_state, 'tensor', axis=0, tiled=True)  10.6 us
  transfers between devices with their start and end apart: 3, of which 3 were waited for; matrix products, arithmetic and copies ran while one was open for 3% of the time, Pallas kernels for 0%

commit v1 on v0

--- a/solution.py
+++ b/solution.py
@@ -1,3 +1,4 @@
+import functools
 import jax
 import jax.numpy as jnp
 from jax import lax
@@ -5,6 +6,17 @@
 
 HEAD_DIM = 64
 epsilon = 1e-06
+
+
+def enter_turns(own_rows, link_axis):
+    inter = own_rows
+    how_many = lax.axis_size(link_axis)
+    for dd in [[(ii, ii ^ k) for ii in range(how_many)] for k in (1, 2, 4, 8, 16) if k < how_many]:
+        inter = inter + lax.ppermute(inter, link_axis, dd)
+    return inter
+
+
+show_core_over_axis = functools.partial(enter_turns, link_axis="tensor")
 
 
 def partner(block, axis, distance):
@@ -119,7 +131,7 @@
     audio_mid = audio_state + audio_modulation[2] * audio_term
     audio_inner_own = modulate(audio_mid, audio_modulation, 3)
     partial_term = jnp.dot(video_mixed, video_output, preferred_element_type=jnp.float32)
-    full_term = lax.psum(partial_term, "tensor")
+    full_term = show_core_over_axis(partial_term)
     video_mid_whole = video_whole + video_modulation[2] * full_term
     video_inner = modulate(video_mid_whole, video_modulation, 3)
     first_row = lax.axis_index("tensor") * video_count

time: 304 us -> 376 us (1.24)
  blocking collectives: 45.4 us -> 78.8 us
  waiting for transfers between devices: 199 us -> 226 us
  other arithmetic: 12 us -> 21.7 us
  starting transfers between devices: 0.12 us -> 4.17 us
    psum x1 -> x0, waiting for transfers between devices: 93.9 us -> none  [on_device(): full_term = lax.psum(partial_term, 'tensor')]
    unnamed x4 -> x5, waiting for transfers between devices: 94.1 us -> 188 us
    all_gather x1, blocking collectives: 21.4 us -> 54.8 us  [on_device(): audio_inner = lax.all_gather(audio_inner_own, 'tensor', axis=0, tiled=True)]
    ppermute x0 -> x4, waiting for transfers between devices: none -> 26.3 us  [enter_turns(): inter = inter + lax.ppermute(inter, link_axis, dd)]
    add x0 -> x3, other arithmetic: none -> 7.96 us  [enter_turns(): inter = inter + lax.ppermute(inter, link_axis, dd)]
    ppermute x0 -> x4, starting transfers between devices: none -> 4.05 us  [enter_turns(): inter = inter + lax.ppermute(inter, link_axis, dd)]
  transfers between devices with their start and end apart: 3 -> 7, of which waited for: 3 -> 5; matrix products, arithmetic and copies ran while one was open for 3% -> 5% of each run, Pallas kernels for 0% -> 0%
where the time goes in v1:
time: 376 us; the launch traced here: 375 us
  waiting for transfers between devices  226 us (60%)
  blocking collectives  78.8 us (21%)
  matrix products  24.1 us (6%)
  other arithmetic  21.7 us (6%)
  between operations  14.7 us (4%)
  local copies, waits for them, and re-layouts  5.86 us (2%)
  starting transfers between devices  4.17 us (1%)
    unnamed x5, waiting for transfers between devices  188 us
    all_gather x1, blocking collectives, on_device(): audio_inner = lax.all_gather(audio_inner_own, 'tensor', axis=0, tiled=True)  54.8 us
    ppermute x4, waiting for transfers between devices, enter_turns(): inter = inter + lax.ppermute(inter, link_axis, dd)  26.3 us
    all_gather x1, blocking collectives, on_device(): audio_normed = lax.all_gather(audio_own, 'tensor', axis=0, tiled=True)  24 us
    dot_general x2, matrix products, feed_rows(): return jnp.dot(hidden, shrink, preferred_element_type=jnp.float32)  13.6 us
    all_gather x1, waiting for transfers between devices, on_device(): video_whole = lax.all_gather(video_state, 'tensor', axis=0, tiled=True)  11.6 us
    add x3, other arithmetic, enter_turns(): inter = inter + lax.ppermute(inter, link_axis, dd)  7.96 us
  transfers between devices with their start and end apart: 7, of which 5 were waited for; matrix products, arithmetic and copies ran while one was open for 5% of the time, Pallas kernels for 0%

profile of v1, /device:TPU:0, one launch (start us, length us, event | category | flops | bytes accessed | tf_op | source)
XLA Modules:
  0.0 375.1 jit_solution(5204745635491179834)
XLA Ops:
  7.2 0.7 all-gather.5.cloned.1.call-update
  8.0 1.7 fusion.80
  9.7 0.9 multiply_reduce_fusion.7
  10.6 0.8 fusion.54
  11.5 24.0 %all-gather.1 = bf16[16,4,2048]{2,1,0:T(4,128)(2,1)S(1)} all-gather(bf16[1,4,2048]{2,1,0:T(4,128)(2,1)S(1)} %fusion.54), channel_id=1, replica_groups=mesh['groups'=2,'tensor'=16] {'tensor'}, dimensions={0}, use_global_device_ids=true | all-gather | bytes 278528 | tf_op jit(solution)/shard_map/all_gather | solution.py:125
  35.5 1.5 convolution_convert_fusion.2
  37.2 0.7 copy.50
  38.7 0.7 fusion.79
  39.4 11.6 %all-gather.5.cloned.1.call-done = f32[16,4,4096]{2,1,0:T(4,128)} async-done(((f32[1,4,4096]{2,1,0:T(4,128)}), f32[16,4,4096]{2,1,0:T(4,128)}) %all-gather.5.cloned.1.call-update) | async-done | bytes 1048592 | tf_op jit(solution)/shard_map/all_gather | solution.py:123
  50.9 1.6 reshape.111
  53.3 2.2 fusion.8
  55.5 0.9 reshape.106
  56.5 1.0 multiply_convert_fusion.2
  57.6 0.9 convolution_convert_fusion.1
  58.5 2.6 fusion.83
  61.9 2.3 collective-permute-done
  64.2 2.7 add.183
  68.4 24.0 %collective-permute-done.1 = f32[64,4096]{1,0:T(8,128)} collective-permute-done((f32[64,4096]{1,0:T(8,128)}, f32[64,4096]{1,0:T(8,128)}, u32[]{:S(2)}, u32[]{:S(2)}) %collective-permute-start.1) | collective-permute-done | bytes 1048608 | tf_op jit(solution)/shard_map/ppermute | solution.py:15
  92.4 2.7 add.184
  96.0 2.1 fusion.84
  99.4 89.4 %all-reduce.7.cloned.1.call-done = f32[64,2048]{1,0:T(8,128)} async-done(((f32[64,2048]{1,0:T(8,128)}), f32[64,2048]{1,0:T(8,128)}) %all-reduce.7.cloned.1.call-update) | async-done | bytes 524304
  188.8 1.0 multiply_reduce_fusion.6
  189.8 2.7 add.185
  192.5 2.9 collective-permute-start.3
  195.5 54.8 %all-gather.2 = bf16[16,4,2048]{2,1,0:T(4,128)(2,1)} all-gather(bf16[1,4,2048]{2,1,0:T(4,128)(2,1)S(1)} %fusion.55), channel_id=1, replica_groups=mesh['groups'=2,'tensor'=16] {'tensor'}, dimensions={0}, use_global_device_ids=true | all-gather | bytes 278528 | tf_op jit(solution)/shard_map/all_gather | solution.py:139
  250.3 1.0 reshape.115
  251.3 3.3 fusion.37
  254.7 2.8 multiply_reduce_fusion
  257.6 10.3 %fusion.24 = f32[64,4096]{1,0:T(8,128)} fusion(bf16[1024,4096]{1,0:T(8,128)(2,1)} %param.25, bf16[4096,1024]{1,0:T(8,128)(2,1)} %param.24, f32[64,4096]{1,0:T(8,128)} %get-tuple-element.7, f32[4096]{0:T(1024)S(1)} %bitcast.60, f32[4096]{0:T(1024)S(1)} %bitcast.61, f32[64]{0:T(128)S(1)} %add_rsqrt_fusion.5), kind=kOutput, calls=%fused_computation.35 | convolution fusion | flops 1075380224 | bytes 18907392 | tf_op jit(solution)/shard_map/dot_general | solution.py:102
  267.8 97.7 %all-reduce.9.cloned.1.call-done = (f32[64,4096]{1,0:T(8,128)}, f32[64,2048]{1,0:T(8,128)}) async-done(((f32[64,4096]{1,0:T(8,128)}, f32[64,2048]{1,0:T(8,128)}), (f32[64,4096]{1,0:T(8,128)}, f32[64,2048]{1,0:T(8,128)})) %all-reduce.9.cloned.1.call-update) | async-done | bytes 1572880
  365.5 1.5 fusion.44
  367.0 1.6 fusion.39
  (76 shorter events, 6.0 us)
Async XLA Ops:
  7.2 244.1 %copy-start = (bf16[512,2048]{1,0:T(8,128)(2,1)S(1)}, bf16[512,2048]{1,0:T(8,128)(2,1)}, u32[]{:S(2)}) copy-start(bf16[512,2048]{1,0:T(8,128)(2,1)} %param.27) | copy-start | bytes 6291460
  7.2 31.5 %copy-start.3 = (f32[6,4096]{1,0:T(8,128)S(1)}, f32[6,4096]{1,0:T(8,128)}, u32[]{:S(2)}) copy-start(f32[6,4096]{1,0:T(8,128)} %param.16) | copy-start | bytes 294916
  7.2 43.7 %all-gather.5.cloned.1.call-start = ((), (), s32[]{:S(2)}) async-start(), calls=%async_computation | async-start | bytes 1114112 | tf_op jit(solution)/shard_map/all_gather | solution.py:123
  7.9 180.9 %all-reduce.7.cloned.1.call-start = ((), (), s32[]{:S(2)}) async-start(), calls=%async_computation.1 | async-start | bytes 1048576
  39.4 13.3 %copy-start.4 = (f32[1,4096]{1,0:T(1,128)}, f32[1,4096]{1,0:T(1,128)S(1)}, u32[]{:S(2)}) copy-start(f32[1,4096]{1,0:T(1,128)S(1)} %get-tuple-element.9) | copy-start | bytes 49156
  39.4 13.4 %copy-start.6 = (f32[1,4096]{1,0:T(1,128)}, f32[1,4096]{1,0:T(1,128)S(1)}, u32[]{:S(2)}) copy-start(f32[1,4096]{1,0:T(1,128)S(1)} %get-tuple-element.10) | copy-start | bytes 49156
  52.7 0.6 copy-start.15
  58.5 2.9 copy-start.1
  61.2 6.1 %copy-start.5 = (f32[1,4096]{1,0:T(1,128)S(1)}, f32[1,4096]{1,0:T(1,128)}, u32[]{:S(2)}) copy-start(f32[1,4096]{1,0:T(1,128)} %copy-done.4) | copy-start | bytes 49156
  61.2 6.1 %copy-start.7 = (f32[1,4096]{1,0:T(1,128)S(1)}, f32[1,4096]{1,0:T(1,128)}, u32[]{:S(2)}) copy-start(f32[1,4096]{1,0:T(1,128)} %copy-done.6) | copy-start | bytes 49156
  61.2 6.1 %copy-start.16 = (f32[64]{0:T(128)S(1)}, f32[64]{0:T(128)}, u32[]{:S(2)}) copy-start(f32[64]{0:T(128)} %copy-done.15) | copy-start | bytes 772
  61.2 3.0 collective-permute-start
  61.7 5.6 %copy-start.17 = (bf16[4096,2,128]{2,1,0:T(2,128)(2,1)S(1)}, bf16[4096,2,128]{2,1,0:T(2,128)(2,1)}, u32[]{:S(2)}) copy-start(bf16[4096,2,128]{2,1,0:T(2,128)(2,1)} %param.22) | copy-start | bytes 6291460
  66.8 25.6 %collective-permute-start.1 = (f32[64,4096]{1,0:T(8,128)}, f32[64,4096]{1,0:T(8,128)}, u32[]{:S(2)}, u32[]{:S(2)}) collective-permute-start(f32[64,4096]{1,0:T(8,128)} %add.183), channel_id=1, source_target_pairs={{0,2},{1,3},{2,0},{3,1},{4,6},{5,7},{6,4},{7,5},{8,10},{9,11},{10,... | collective-permute-start | bytes 3145736 | tf_op jit(solution)/shard_map/ppermute | solution.py:15
  68.3 29.8 %copy-start.18 = (u32[32]{0:T(128)S(1)}, u32[32]{0:T(128)}, u32[]{:S(2)}) copy-start(u32[32]{0:T(128)} %constant.50) | copy-start | bytes 388
  68.3 120.5 %copy-start.2 = (f32[4,2048]{1,0:T(4,128)S(1)}, f32[4,2048]{1,0:T(4,128)}, u32[]{:S(2)}) copy-start(f32[4,2048]{1,0:T(4,128)} %param.15) | copy-start | bytes 98308
  68.4 120.5 %copy-start.14 = (f32[1,2048]{1,0:T(1,128)S(1)}, f32[1,2048]{1,0:T(1,128)}, u32[]{:S(2)}) copy-start(f32[1,2048]{1,0:T(1,128)} %get-tuple-element.15) | copy-start | bytes 24580
  95.1 94.8 %collective-permute-start.2 = (f32[64,4096]{1,0:T(8,128)}, f32[64,4096]{1,0:T(8,128)}, u32[]{:S(2)}, u32[]{:S(2)}) collective-permute-start(f32[64,4096]{1,0:T(8,128)} %add.184), channel_id=1, source_target_pairs={{0,4},{1,5},{2,6},{3,7},{4,0},{5,1},{6,2},{7,3},{8,12},{9,13},{10,... | collective-permute-start | bytes 3145736 | tf_op jit(solution)/shard_map/ppermute | solution.py:15
  98.1 97.3 %copy-start.12 = (f32[1,2048]{1,0:T(1,128)S(1)}, f32[1,2048]{1,0:T(1,128)}, u32[]{:S(2)}) copy-start(f32[1,2048]{1,0:T(1,128)} %get-tuple-element.18) | copy-start | bytes 24580
  98.1 97.3 %copy-start.13 = (f32[1,2048]{1,0:T(1,128)S(1)}, f32[1,2048]{1,0:T(1,128)}, u32[]{:S(2)}) copy-start(f32[1,2048]{1,0:T(1,128)} %get-tuple-element.19) | copy-start | bytes 24580
  98.1 267.4 %all-reduce.9.cloned.1.call-start = ((), (), s32[]{:S(2)}) async-start(), calls=%async_computation.2 | async-start | bytes 3145728
  192.5 62.2 %collective-permute-start.3 = (f32[64,4096]{1,0:T(8,128)}, f32[64,4096]{1,0:T(8,128)}, u32[]{:S(2)}, u32[]{:S(2)}) collective-permute-start(f32[64,4096]{1,0:T(8,128)} %add.185), channel_id=1, source_target_pairs={{0,8},{1,9},{2,10},{3,11},{4,12},{5,13},{6,14},{7,15},{8,0},{9,1},... | collective-permute-start | bytes 3145736 | tf_op jit(solution)/shard_map/ppermute | solution.py:15
  254.7 2.9 copy-start.9
  254.7 2.9 copy-start.10
  257.5 108.0 %copy-start.11 = (f32[1,2048]{1,0:T(1,128)S(1)}, f32[1,2048]{1,0:T(1,128)}, u32[]{:S(2)}) copy-start(f32[1,2048]{1,0:T(1,128)} %get-tuple-element.14) | copy-start | bytes 24580
  257.5 109.4 %copy-start.8 = (f32[1,4096]{1,0:T(1,128)S(1)}, f32[1,4096]{1,0:T(1,128)}, u32[]{:S(2)}) copy-start(f32[1,4096]{1,0:T(1,128)} %get-tuple-element.8) | copy-start | bytes 49156
Sparse Core Ops, SparseCore 0:
  10.2 40.7 all-gather.4
  98.2 90.5 all-reduce.6
  267.9 97.5 all-reduce.8
